TPU v7x, 32 devices: a whole 2x2x4 slice. The times are simulated.
32 devices in a mesh: dp: 4 (over x, core), tensor: 8 (over z, y).
Axes of the slice: x: 2, y: 2, z: 4, core: 2. Of those that a mesh axis runs over, the one named last changes fastest.
Arguments:
- out_grad: bfloat16 [2, 320, 4096], P(None, 'dp', 'tensor'), may hold values from -0.3125 to 0.3125
- layer_input: bfloat16 [2, 320, 4096], P(None, 'dp', 'tensor'), may hold values from -8 to 8
- w_down: bfloat16 [16384, 4096], P('tensor'), may hold values from -0.046875 to 0.046875
- silu_gate: bfloat16 [2, 320, 16384], P(None, 'dp', 'tensor'), may hold values from -6 to 6
- up_proj: bfloat16 [2, 320, 16384], P(None, 'dp', 'tensor'), may hold values from -6 to 6
- slope_codes: int32 [2, 32, 16384], P(None, 'dp', 'tensor'), may hold values from 0 to 1073741823
Outputs:
- grad_down: bfloat16 [16384, 4096], P('tensor', 'dp')
- grad_gate: bfloat16 [4096, 16384], P('dp', 'tensor')
- grad_up: bfloat16 [4096, 16384], P('dp', 'tensor')
Inputs may be any that keep to these rules, and one draw needn't show every extreme that they name: `slope_codes`: every word holds ten independent 3-bit codes; all eight codes occur.
All inputs are finite; a program needn't handle non-finite values.
Results may differ from a plain program's by a relative error of at most 0.018.
Values may be sent and summed in bfloat16 or wider, within the bound.
A program may use at most 128 MiB of HBM per device.

v0:
```python
import jax
import jax.numpy as jnp
from jax import lax
from jax.sharding import PartitionSpec as P

SLOPE_LEVELS = (-0.09, 0.06, 0.22, 0.41, 0.6, 0.79, 0.96, 1.08)


def decode_slopes(packed):
    shifts = 3 * jnp.arange(10, dtype=jnp.int32)
    pieces = jnp.bitwise_and(jnp.right_shift(packed[..., None, :], shifts[:, None]), 7)
    pieces = pieces.reshape(packed.shape[:-2] + (packed.shape[-2] * 10, packed.shape[-1]))
    result = jnp.full(pieces.shape, SLOPE_LEVELS[0], jnp.float32)
    for symbol in range(1, 8):
        result = jnp.where(pieces == symbol, jnp.float32(SLOPE_LEVELS[symbol]), result)
    return result


def shards(out_grad, layer_input, w_down, silu_gate, up_proj, slope_codes):
    micro_count = out_grad.shape[0]
    model_width = w_down.shape[1]
    hidden_width = w_down.shape[0]
    group_rows = micro_count * out_grad.shape[1]
    grad_rows, input_rows = (
        lax.all_gather(out_grad, "tensor", axis=2, tiled=True),
        lax.all_gather(layer_input, "tensor", axis=2, tiled=True),
    )
    output_all = grad_rows.reshape(-1, model_width)
    input_all = input_rows.reshape(-1, model_width)
    gate_act = silu_gate.reshape(-1, hidden_width).astype(jnp.float32)
    up_value = up_proj.reshape(-1, hidden_width).astype(jnp.float32)
    hidden = (gate_act * up_value).astype(jnp.bfloat16)
    slopes = decode_slopes(slope_codes).reshape(-1, hidden_width)
    hidden_grad = lax.dot_general(
        output_all, w_down, (((1,), (1,)), ((), ())), preferred_element_type=jnp.float32
    )
    up_grad = (hidden_grad * gate_act).astype(jnp.bfloat16)
    gate_grad = (hidden_grad * up_value * slopes).astype(jnp.bfloat16)
    block_inputs, block_outputs = (
        lax.all_to_all(input_all, "dp", split_axis=1, concat_axis=0, tiled=True),
        lax.all_to_all(output_all, "dp", split_axis=1, concat_axis=0, tiled=True),
    )
    activations = jnp.concatenate((gate_grad, up_grad, hidden), axis=1)
    values = lax.all_gather(activations, "dp", axis=0, tiled=True)
    row_count = values.shape[0]
    groups = row_count // group_rows
    inputs_3d = block_inputs.reshape(groups, group_rows, block_inputs.shape[1])
    outputs_3d = block_outputs.reshape(groups, group_rows, block_outputs.shape[1])
    values_3d = values.reshape(groups, group_rows, values.shape[1])
    gate_up_parts = jnp.einsum(
        "grd,grf->gdf",
        inputs_3d,
        values_3d[:, :, : 2 * hidden_width],
        preferred_element_type=jnp.float32,
    )
    down_parts = jnp.einsum(
        "grf,grd->gfd",
        values_3d[:, :, 2 * hidden_width :],
        outputs_3d,
        preferred_element_type=jnp.float32,
    )
    gate_up_sum = jnp.sum(gate_up_parts.astype(jnp.bfloat16).astype(jnp.float32), axis=0)
    down_sum = jnp.sum(down_parts.astype(jnp.bfloat16).astype(jnp.float32), axis=0)
    grad_down = down_sum.astype(jnp.bfloat16)
    grad_gate = gate_up_sum[:, :hidden_width].astype(jnp.bfloat16)
    grad_up = gate_up_sum[:, hidden_width:].astype(jnp.bfloat16)
    return (grad_down, grad_gate, grad_up)


def solution(mesh):
    return jax.shard_map(
        shards,
        mesh=mesh,
        in_specs=(
            P(None, "dp", "tensor"),
            P(None, "dp", "tensor"),
            P("tensor", None),
            P(None, "dp", "tensor"),
            P(None, "dp", "tensor"),
            P(None, "dp", "tensor"),
        ),
        out_specs=(P("tensor", "dp"), P("dp", "tensor"), P("dp", "tensor")),
        check_vma=False,
    )
```

profile of v0, /device:TPU:0, one launch (start us, length us, event | category | flops | bytes accessed | tf_op | source)
XLA Modules:
  0.0 234.2 jit_solution(13841438188736707465)
XLA Ops:
  7.2 0.0 all-gather.4.cloned.1.call-start
  7.2 0.7 all-gather.4.cloned.1.call-update
  7.9 0.0 all-gather.8.cloned.1.call-start
  7.9 0.7 all-gather.8.cloned.1.call-update
  8.6 0.0 all-gather.6.cloned.1.call-start
  8.7 0.1 shift_right_arithmetic.28
  8.8 0.1 shift_right_arithmetic.30
  8.9 1.1 shift_right_arithmetic.25
  10.0 0.2 shift_right_arithmetic.26
  10.2 44.1 %all-gather.4.cloned.1.call-done = bf16[2,80,4096]{2,1,0:T(8,128)(2,1)} async-done(((bf16[2,80,512]{2,1,0:T(8,128)(2,1)}), bf16[2,80,4096]{2,1,0:T(8,128)(2,1)}) %all-gather.4.cloned.1.call-update) | async-done | bytes 1310736 | tf_op jit(solution)/shard_map/all_gather | solution.py:25
  54.3 12.8 %fusion.4 = (bf16[160,2048]{1,0:T(8,128)(2,1)S(1)}, bf16[160,2048]{1,0:T(8,128)(2,1)S(1)}, bf16[160,2048]{1,0:T(8,128)(2,1)S(1)}) fusion(s32[160,2048]{1,0:T(8,128)S(1)} %shift_right_arithmetic.26, bf16[2,80,2048]{2,1,0:T(8,128)(2,1)} %param.10, s32[160]{0:T(256)S(1)} %shift_right_arithmetic.30, bf16[2,80,2048]{2,1,0:T(8,128)(2,1)} %param.9, ...), kind=kOutput, calls=%fused_computation.10 | convolution fusion | flops 2692546560 | bytes 22676096 | tf_op jit(solution)/shard_map/dot_general | solution.py:34
  67.1 1.4 pad_maximum_fusion
  68.5 0.0 all-gather.6.cloned.1.call-update
  68.5 27.8 %all-gather.8.cloned.1.call-done = bf16[2,80,4096]{2,1,0:T(8,128)(2,1)} async-done(((bf16[2,80,512]{2,1,0:T(8,128)(2,1)}), bf16[2,80,4096]{2,1,0:T(8,128)(2,1)}) %all-gather.8.cloned.1.call-update) | async-done | bytes 1310736 | tf_op jit(solution)/shard_map/all_gather | solution.py:26
  96.3 3.2 %all_to_all.27 = bf16[160,4,1024]{2,1,0:T(4,128)(2,1)S(1)} reshape(bf16[2,80,4096]{2,1,0:T(8,128)(2,1)} %all-gather.8.cloned.1.call-done) | data formatting | bytes 2621440 | tf_op jit(solution)/shard_map/all_to_all | solution.py:40
  99.5 1.4 copy.12
  101.0 0.0 copy-start
  101.0 4.5 %all-to-all-start.1 = ((bf16[160,4,1024]{2,0,1:T(8,128)(2,1)}), bf16[160,4,1024]{2,0,1:T(8,128)(2,1)}, u32[]{:S(2)}, u32[]{:S(2)}) async-start(bf16[160,4,1024]{2,0,1:T(8,128)(2,1)} %copy.12), calls=%async_computation.1 | async-start | bytes 2621440 | tf_op jit(solution)/shard_map/all_to_all | solution.py:40
  105.5 0.0 copy-done
  105.5 1.0 all_to_all.24
  106.5 1.5 copy.11
  108.0 29.0 %all-to-all-done.1 = bf16[160,4,1024]{2,0,1:T(8,128)(2,1)} async-done(((bf16[160,4,1024]{2,0,1:T(8,128)(2,1)}), bf16[160,4,1024]{2,0,1:T(8,128)(2,1)}, u32[]{:S(2)}, u32[]{:S(2)}) %all-to-all-start.1) | async-done | bytes 1310752 | tf_op jit(solution)/shard_map/all_to_all | solution.py:40
  137.0 3.7 %all-to-all-start = ((bf16[160,4,1024]{2,0,1:T(8,128)(2,1)}), bf16[160,4,1024]{2,0,1:T(8,128)(2,1)S(1)}, u32[]{:S(2)}, u32[]{:S(2)}) async-start(bf16[160,4,1024]{2,0,1:T(8,128)(2,1)} %copy.11), calls=%async_computation | async-start | bytes 2621440 | tf_op jit(solution)/shard_map/all_to_all | solution.py:41
  140.8 39.4 %all-gather.6.cloned.1.call-done = bf16[640,6144]{1,0:T(8,128)(2,1)} async-done(((bf16[160,6144]{1,0:T(8,128)(2,1)}), bf16[640,6144]{1,0:T(8,128)(2,1)}) %all-gather.6.cloned.1.call-update) | async-done | bytes 7864336 | tf_op jit(solution)/shard_map/all_gather | solution.py:44
  180.2 19.0 %convert_reduce_fusion = bf16[4096,1024]{1,0:T(8,128)(2,1)} fusion(bf16[4,160,6144]{2,1,0:T(8,128)(2,1)} %bitcast.21, bf16[160,4,1024]{2,0,1:T(8,128)(2,1)} %all-to-all-done.1), kind=kOutput, calls=%fused_computation | convolution fusion | flops 5398069248 | bytes 14942208 | tf_op jit(solution)/shard_map/grd,grf->gdf/dot_general | solution.py:50
  199.2 6.0 %fusion.8 = (bf16[1024,2048]{0,1:T(8,128)(2,1)}, bf16[1024,2048]{0,1:T(8,128)(2,1)}) fusion(bf16[1024,4096]{0,1:T(8,128)(2,1)} %bitcast.19), kind=kLoop, calls=%fused_computation.16 | loop fusion | bytes 16777216 | tf_op jit(solution)/shard_map/slice | solution.py:66
  205.2 6.4 %copy.14 = bf16[1024,2048]{1,0:T(8,128)(2,1)} copy(bf16[1024,2048]{0,1:T(8,128)(2,1)} %get-tuple-element.6) | data formatting | bytes 8388608
  211.6 6.4 %copy.13 = bf16[1024,2048]{1,0:T(8,128)(2,1)} copy(bf16[1024,2048]{0,1:T(8,128)(2,1)} %get-tuple-element.7) | data formatting | bytes 8388608
  218.0 0.0 all-to-all-done
  218.0 9.6 %convert_reduce_fusion.1 = bf16[2048,1024]{1,0:T(8,128)(2,1)} fusion(bf16[4,160,6144]{2,1,0:T(8,128)(2,1)} %bitcast.22, bf16[160,4,1024]{2,0,1:T(8,128)(2,1)S(1)} %all-to-all-done), kind=kOutput, calls=%fused_computation.1 | convolution fusion | flops 2699034624 | bytes 8126464 | tf_op jit(solution)/shard_map/grf,grd->gfd/dot_general | solution.py:56
  (3 shorter events, 0.0 us)
Async XLA Ops:
  7.2 47.2 %all-gather.4.cloned.1.call-start = ((), (), s32[]{:S(2)}) async-start(), calls=%async_computation.2 | async-start | bytes 1474560 | tf_op jit(solution)/shard_map/all_gather | solution.py:25
  7.9 88.4 %all-gather.8.cloned.1.call-start = ((), (), s32[]{:S(2)}) async-start(), calls=%async_computation.4 | async-start | bytes 1474560 | tf_op jit(solution)/shard_map/all_gather | solution.py:26
  8.6 171.5 %all-gather.6.cloned.1.call-start = ((), (), s32[]{:S(2)}) async-start(), calls=%async_computation.3 | async-start | bytes 9830400 | tf_op jit(solution)/shard_map/all_gather | solution.py:44
  101.0 4.5 %copy-start = (bf16[2,80,4096]{2,1,0:T(8,128)(2,1)S(1)}, bf16[2,80,4096]{2,1,0:T(8,128)(2,1)}, u32[]{:S(2)}) copy-start(bf16[2,80,4096]{2,1,0:T(8,128)(2,1)} %all-gather.4.cloned.1.call-done) | copy-start | bytes 3932164
  101.0 36.0 %all-to-all-start.1 = ((bf16[160,4,1024]{2,0,1:T(8,128)(2,1)}), bf16[160,4,1024]{2,0,1:T(8,128)(2,1)}, u32[]{:S(2)}, u32[]{:S(2)}) async-start(bf16[160,4,1024]{2,0,1:T(8,128)(2,1)} %copy.12), calls=%async_computation.1 | async-start | bytes 2621440 | tf_op jit(solution)/shard_map/all_to_all | solution.py:40
  137.0 81.0 %all-to-all-start = ((bf16[160,4,1024]{2,0,1:T(8,128)(2,1)}), bf16[160,4,1024]{2,0,1:T(8,128)(2,1)S(1)}, u32[]{:S(2)}, u32[]{:S(2)}) async-start(bf16[160,4,1024]{2,0,1:T(8,128)(2,1)} %copy.11), calls=%async_computation | async-start | bytes 2621440 | tf_op jit(solution)/shard_map/all_to_all | solution.py:41
Sparse Core Ops, SparseCore 0:
  10.0 44.2 all-gather.3
  56.4 39.8 all-gather.7
  98.4 81.6 all-gather.5
where the time goes:
time: 235 us; the launch traced here: 234 us
  waiting for transfers between devices  142 us (60%)
  matrix products  41.4 us (18%)
  local copies, waits for them, and re-layouts  27.5 us (12%)
  between operations  13.8 us (6%)
  starting transfers between devices  8.34 us (4%)
    all_gather x1, waiting for transfers between devices, shards(): lax.all_gather(out_grad, 'tensor', axis=2, tiled=True)  44.1 us
    all_gather x1, waiting for transfers between devices, shards(): values = lax.all_gather(activations, 'dp', axis=0, tiled=True)  39.4 us
    all_to_all x1, waiting for transfers between devices, shards(): lax.all_to_all(input_all, 'dp', split_axis=1, concat_axis=0, tiled=True)  29 us
    all_gather x1, waiting for transfers between devices, shards(): lax.all_gather(layer_input, 'tensor', axis=2, tiled=True)  27.8 us
    dot_general x1, matrix products, shards(): jnp.einsum('grd,grf->gdf', inputs_3d, values_3d[:, :, :2 * hidden_width],...  19 us
    unnamed x4, local copies, waits for them, and re-layouts  12.8 us
    dot_general x1, matrix products, shards(): lax.dot_general(output_all, w_down, (((1,), (1,)), ((), ())), preferred_e...  12.8 us
    dot_general x1, matrix products, shards(): jnp.einsum('grf,grd->gfd', values_3d[:, :, 2 * hidden_width:], outputs_3d...  9.61 us
  transfers between devices with their start and end apart: 5, of which 4 were waited for; matrix products, arithmetic and copies ran while one was open for 24% of the time, Pallas kernels for 0%

commit v1 on v0

v1 whole, which is shorter than its diff:
```python
import functools

import jax
import jax.numpy as jnp
from jax import lax
from jax.experimental import pallas as pl
from jax.experimental.pallas import tpu as pltpu
from jax.sharding import PartitionSpec as P

SLOPE_LEVELS = (-0.09, 0.06, 0.22, 0.41, 0.6, 0.79, 0.96, 1.08)
MESH = pl.DeviceIdType.MESH
CHUNKS = 4


def exchange(n_dp, n_t, out_ref, in_ref, silu_ref, up_ref, code_ref, spread_ref, w_ref,
             xg, hid_all, gate_all, up_all,
             og, wbuf, vbuf, own, stage,
             w_sem, p_send, p_recv, py_send, py_recv, og_sem,
             s_send, s_recv, h_send, h_sem, c_recv, zu_send, zd_send, y_send, y_recv,
             o_sem, o_send, o_recv, al_sem, ax_send, ax_recv, ac_send, ac_recv):
    chips = n_dp // 2
    rows = n_t // 2
    ratio = n_t // n_dp
    tokens, cols = out_ref.shape
    width = w_ref.shape[1]
    hidden = w_ref.shape[0]
    block = width // n_dp
    fc = hidden // CHUNKS
    units = 2 + 4 * (chips - 1)
    all_acts = (hid_all, gate_all, up_all)

    d = lax.axis_index("dp")
    t = lax.axis_index("tensor")
    q, c = d // 2, lax.rem(d, 2)
    z, y = t // 2, lax.rem(t, 2)
    partner = q * 2 + (1 - c)
    y_peer = z * 2 + (1 - y)
    owner = t // ratio
    owner_chip = owner // 2
    if ratio == 2:
        in_chain = d >= 0
        has_side = d >= 0
        chain_col, side_col = y, 1 - y
    else:
        in_chain = lax.rem(d, 2) == y
        has_side = lax.rem(d, 2) != y
        chain_col, side_col = y * 0, y * 0
    head_row = (d * ratio) // 2

    def chip_at(r):
        return lax.rem(q + r, chips) * 2 + c

    def row_at(k):
        return lax.rem(z + k, rows) * 2 + y

    def group_from(r, core):
        return lax.rem(q + chips - r, chips) * 2 + core

    def at_col(index, size):
        return pl.ds(pl.multiple_of(index * size, 128), size)

    def remote(src, dst, send, recv, dp, tensor):
        return pltpu.make_async_remote_copy(
            src_ref=src, dst_ref=dst, send_sem=send, recv_sem=recv,
            device_id={"dp": dp, "tensor": tensor}, device_id_type=MESH)

    barrier = pltpu.get_barrier_semaphore()
    greet = [(d, row_at(k)) for k in range(1, rows)] + [(d, y_peer), (partner, t)]
    greet += [(chip_at(r), t) for r in range(1, chips)]
    for dp, tensor in greet:
        pl.semaphore_signal(barrier, inc=1, device_id={"dp": dp, "tensor": tensor}, device_id_type=MESH)
    pl.semaphore_wait(barrier, len(greet))

    my_cols = og.at[:, at_col(t, cols)]

    def row_copy(k):
        return remote(out_ref, my_cols, p_send.at[k - 1], p_recv.at[k - 1], d, row_at(k))

    def row_wait(k):
        src = lax.rem(z + rows - k, rows) * 2 + y
        land = og.at[:, at_col(src, cols)]
        return remote(land, land, p_send.at[k - 1], p_recv.at[k - 1], d, y_peer)

    def side_copy(k):
        src = lax.rem(z + rows - k, rows) * 2 + y
        piece = og.at[:, at_col(src, cols)]
        return remote(out_ref if k == 0 else piece, piece, py_send.at[k], py_recv.at[k], d, y_peer)

    def side_wait(k):
        src = lax.rem(z + rows - k, rows) * 2 + (1 - y)
        piece = og.at[:, at_col(src, cols)]
        return remote(piece, piece, py_send.at[k], py_recv.at[k], d, y_peer)

    for k in range(1, rows):
        row_copy(k).start()
    side_copy(0).start()
    og_own = pltpu.make_async_copy(out_ref, my_cols, og_sem)
    og_own.start()

    away = owner_chip != q
    dist = lax.rem(owner_chip + chips - q, chips)
    slot = lax.max(dist - 1, 0)
    far = owner_chip * 2 + c

    def cross(a):
        src = in_ref if a == 0 else out_ref
        return remote(src, stage.at[a, slot], s_send.at[a], s_recv.at[a, slot], far, t)

    @pl.when(away)
    def _():
        for a in range(2):
            cross(a).start()

    def w_copy(j):
        part = pl.ds(pl.multiple_of(j * fc, 128), fc)
        return pltpu.make_async_copy(w_ref.at[part], wbuf.at[part], w_sem.at[j])

    for j in range(CHUNKS):
        w_copy(j).start()

    def unit_of(r, a):
        return 0 if r == 0 else 2 + (r - 1) * 4 + a * 2

    def hand(r, a, to_self):
        src = in_ref if r == 0 else stage.at[a, r - 1]
        u = unit_of(r, a) + c
        i = 0 if r == 0 else 1 + (r - 1) * 2 + a
        dst = xg.at[a, group_from(r, c), :, at_col(chain_col if ratio == 2 else 0, cols)]
        if to_self:
            return pltpu.make_async_copy(src, dst, c_recv.at[u])
        return remote(src, dst, h_send.at[i], c_recv.at[u], partner, t)

    source = owner_chip == q
    self_head = jnp.logical_and(source, owner == d)
    other_head = jnp.logical_and(source, owner != d)

    def hand_start(r, a):
        @pl.when(self_head)
        def _():
            hand(r, a, True).start()

        @pl.when(other_head)
        def _():
            hand(r, a, False).start()

    hand_start(0, 0)

    def f_part(j):
        return pl.ds(pl.multiple_of(j * fc, 128), fc)

    def own_local(a, j):
        return pltpu.make_async_copy(
            own.at[a, :, f_part(j)], all_acts[a].at[d, :, f_part(j)], al_sem.at[a, j])

    def own_chip(a, j, r):
        return remote(own.at[a, :, f_part(j)], all_acts[a].at[d, :, f_part(j)],
                      ax_send.at[a, r - 1, j], ax_recv.at[a, r - 1, j], chip_at(r), t)

    def own_core(a, j):
        return remote(own.at[a, :, f_part(j)], all_acts[a].at[d, :, f_part(j)],
                      ac_send.at[a, 0, j], ac_recv.at[a, 0, j], partner, t)

    def pass_core(a, j, r):
        land = all_acts[a].at[group_from(r, c), :, f_part(j)]
        return remote(land, land, ac_send.at[a, r, j], ac_recv.at[a, r, j], partner, t)

    def chip_wait(a, j, r):
        land = all_acts[a].at[group_from(r, c), :, f_part(j)]
        return remote(land, land, ax_send.at[a, r - 1, j], ax_recv.at[a, r - 1, j], partner, t)

    def core_wait(a, j, r):
        land = all_acts[a].at[group_from(r, 1 - c), :, f_part(j)]
        return remote(land, land, ac_send.at[a, r, j], ac_recv.at[a, r, j], partner, t)

    def send_own(a, j):
        for r in range(1, chips):
            own_chip(a, j, r).start()
        own_core(a, j).start()
        own_local(a, j).start()

    def early(j, carry):
        f = f_part(j)
        up_value = up_ref[:, f].astype(jnp.float32)
        own[0, :, f] = (silu_ref[:, f].astype(jnp.float32) * up_value).astype(jnp.bfloat16)
        words = code_ref[:, f]
        pieces = jnp.concatenate(
            [((words >> (3 * k)) & 7).astype(jnp.float32).astype(jnp.bfloat16) for k in range(10)], axis=0)
        symbols = jnp.dot(spread_ref[...], pieces, preferred_element_type=jnp.float32)
        slopes = jnp.full(symbols.shape, SLOPE_LEVELS[0], jnp.float32)
        for s in range(1, 8):
            slopes = jnp.where(symbols > s - 0.5, jnp.float32(SLOPE_LEVELS[s]), slopes)
        vbuf[:, f] = up_value * slopes
        send_own(0, j)
        return carry

    lax.fori_loop(0, CHUNKS, early, 0)

    for k in range(1, rows):
        row_wait(k).wait_recv()
        side_copy(k).start()

    for a in range(2):
        for r in range(1, chips):
            @pl.when(source)
            def _():
                land = stage.at[a, r - 1]
                remote(land, land, s_send.at[a], s_recv.at[a, r - 1], partner, t).wait_recv()
            hand_start(r, a)

    og_own.wait()
    for k in range(rows):
        side_wait(k).wait_recv()

    o_own = pltpu.make_async_copy(og.at[:, at_col(d, block)], xg.at[1, d], o_sem)
    o_own.start()
    o_other = remote(og.at[:, at_col(partner, block)], xg.at[1, d], o_send, o_recv, partner, t)
    o_other.start()

    go_up = jnp.logical_and(in_chain, jnp.logical_and(z >= head_row, z + 1 < rows))
    go_down = jnp.logical_and(in_chain, jnp.logical_and(z <= head_row, z > 0))
    z_up = lax.min(z + 1, rows - 1) * 2 + y
    z_down = lax.max(z - 1, 0) * 2 + y

    def unit_ref(u, col):
        v = lax.max(u - 2, 0)
        far_unit = u >= 2
        r = jnp.where(far_unit, v // 4 + 1, 0)
        a = jnp.where(far_unit, lax.rem(v // 2, 2), 0)
        core = lax.rem(u, 2)
        return xg.at[a, group_from(r, core), :, at_col(col, cols)]

    def chain(u):
        piece = unit_ref(u, chain_col)
        return (remote(piece, piece, zu_send.at[u], c_recv.at[u], d, z_up),
                remote(piece, piece, zd_send.at[u], c_recv.at[u], d, z_down),
                remote(piece, piece, y_send.at[u], y_recv.at[u], d, y_peer))

    def chain_step(u):
        up_copy, down_copy, across = chain(u)

        @pl.when(in_chain)
        def _():
            up_copy.wait_recv()

        @pl.when(go_up)
        def _():
            up_copy.start()

        @pl.when(go_down)
        def _():
            down_copy.start()

        @pl.when(in_chain)
        def _():
            across.start()

    per = -(-units // CHUNKS)

    def late(j, carry):
        f = f_part(j)
        w_copy(j).wait()
        grad = lax.dot_general(og[...], wbuf[f, :], (((1,), (1,)), ((), ())),
                               preferred_element_type=jnp.float32)
        own[1, :, f] = (grad * vbuf[:, f]).astype(jnp.bfloat16)
        own[2, :, f] = (grad * silu_ref[:, f].astype(jnp.float32)).astype(jnp.bfloat16)
        send_own(1, j)
        send_own(2, j)
        for i in range(per):
            u = j * per + i

            @pl.when(u < units)
            def _():
                chain_step(u)
        return carry

    lax.fori_loop(0, CHUNKS, late, 0)

    def relay(a):
        def step(j, carry):
            for r in range(1, chips):
                chip_wait(a, j, r).wait_recv()
                pass_core(a, j, r).start()
            return carry
        return step

    lax.fori_loop(0, CHUNKS, relay(0), 0)

    def relay_late(j, carry):
        relay(1)(j, carry)
        return relay(2)(j, carry)

    lax.fori_loop(0, CHUNKS, relay_late, 0)

    for k in range(1, rows):
        row_copy(k).wait_send()
    for k in range(rows):
        side_copy(k).wait_send()

    @pl.when(away)
    def _():
        for a in range(2):
            cross(a).wait_send()

    @pl.when(other_head)
    def _():
        for r in range(chips):
            for a in range(2):
                if r or not a:
                    hand(r, a, False).wait_send()

    o_own.wait()
    o_other.wait()

    def unit_end(u, carry):
        up_copy, down_copy, across = chain(u)

        @pl.when(go_up)
        def _():
            up_copy.wait_send()

        @pl.when(go_down)
        def _():
            down_copy.wait_send()

        @pl.when(in_chain)
        def _():
            across.wait_send()

        @pl.when(has_side)
        def _():
            piece = unit_ref(u, side_col)
            remote(piece, piece, y_send.at[u], y_recv.at[u], d, y_peer).wait_recv()
        return carry

    lax.fori_loop(0, units, unit_end, 0)

    def act_end(j, carry):
        for a in range(3):
            own_local(a, j).wait()
            own_core(a, j).wait_send()
            core_wait(a, j, 0).wait_recv()
            for r in range(1, chips):
                own_chip(a, j, r).wait_send()
                pass_core(a, j, r).wait_send()
                core_wait(a, j, r).wait_recv()
        return carry

    lax.fori_loop(0, CHUNKS, act_end, 0)


def shards(n_dp, n_t, out_grad, layer_input, w_down, silu_gate, up_proj, slope_codes):
    hidden, width = w_down.shape
    cols = out_grad.shape[2]
    tokens = out_grad.shape[0] * out_grad.shape[1]
    chips, rows, block = n_dp // 2, n_t // 2, width // n_dp
    words = tokens // 10
    row = lax.broadcasted_iota(jnp.int32, (tokens, tokens), 0)
    col = lax.broadcasted_iota(jnp.int32, (tokens, tokens), 1)
    spread = (col == (row % 10) * words + row // 10).astype(jnp.bfloat16)
    units = 2 + 4 * (chips - 1)
    far = chips - 1
    bf16 = jnp.bfloat16
    dma = pltpu.SemaphoreType.DMA
    vmem = pl.BlockSpec(memory_space=pltpu.VMEM)
    anywhere = pl.BlockSpec(memory_space=pl.ANY)
    acts = jax.ShapeDtypeStruct((n_dp, tokens, hidden), bf16)
    flops = 2 * tokens * hidden * width
    xg, hid, gate, up = pl.pallas_call(
        functools.partial(exchange, n_dp, n_t),
        out_shape=(jax.ShapeDtypeStruct((2, n_dp, tokens, block), bf16), acts, acts, acts),
        in_specs=[vmem] * 6 + [anywhere],
        out_specs=[anywhere] * 4,
        scratch_shapes=[
            pltpu.VMEM((tokens, width), bf16),
            pltpu.VMEM((hidden, width), bf16),
            pltpu.VMEM((tokens, hidden), jnp.float32),
            pltpu.VMEM((3, tokens, hidden), bf16),
            pltpu.VMEM((2, far, tokens, cols), bf16),
            dma((CHUNKS,)),
            dma((rows - 1,)), dma((rows - 1,)), dma((rows,)), dma((rows,)), dma,
            dma((2,)), dma((2, far)), dma((1 + 2 * far,)), dma,
            dma((units,)), dma((units,)), dma((units,)), dma((units,)), dma((units,)),
            dma, dma, dma,
            dma((3, CHUNKS)), dma((3, far, CHUNKS)), dma((3, far, CHUNKS)),
            dma((3, chips, CHUNKS)), dma((3, chips, CHUNKS)),
        ],
        compiler_params=pltpu.CompilerParams(
            collective_id=0, has_side_effects=True, vmem_limit_bytes=60 * 1024 * 1024),
        cost_estimate=pl.CostEstimate(flops=flops, bytes_accessed=50_000_000, transcendentals=0),
    )(
        out_grad.reshape(tokens, cols), layer_input.reshape(tokens, cols),
        silu_gate.reshape(tokens, hidden), up_proj.reshape(tokens, hidden),
        slope_codes.reshape(words, hidden), spread, w_down,
    )
    total = n_dp * tokens
    inputs, outputs = xg[0].reshape(total, block), xg[1].reshape(total, block)
    over_rows = (((0,), (0,)), ((), ()))

    def product(left, right):
        return lax.dot_general(left, right, over_rows, preferred_element_type=jnp.float32).astype(bf16)

    return (
        product(hid.reshape(total, hidden), outputs),
        product(inputs, gate.reshape(total, hidden)),
        product(inputs, up.reshape(total, hidden)),
    )


def solution(mesh):
    n_dp, n_t = mesh.shape["dp"], mesh.shape["tensor"]
    return jax.shard_map(
        functools.partial(shards, n_dp, n_t),
        mesh=mesh,
        in_specs=(
            P(None, "dp", "tensor"),
            P(None, "dp", "tensor"),
            P("tensor", None),
            P(None, "dp", "tensor"),
            P(None, "dp", "tensor"),
            P(None, "dp", "tensor"),
        ),
        out_specs=(P("tensor", "dp"), P("dp", "tensor"), P("dp", "tensor")),
        check_vma=False,
    )
```

time: 235 us -> 90.7 us (0.39)
  waiting for transfers between devices: 142 us -> 0 us
  Pallas kernels: 0 us -> 71.5 us
  matrix products: 41.4 us -> 15 us
  local copies, waits for them, and re-layouts: 27.5 us -> 2.52 us
  between operations: 13.8 us -> 0.67 us
  starting transfers between devices: 8.34 us -> 0 us
    all_gather x3 -> x0, waiting for transfers between devices: 111 us -> none  [the longest x1 44.1 us: shards(): lax.all_gather(out_grad, 'tensor', axis=2, tiled=True)]
    pallas_call x0 -> x1, Pallas kernels: none -> 71.5 us  [shards(): pl.pallas_call(functools.partial(exchange, n_dp, n_t), out_shape=(jax.Sha...]
    all_to_all x2 -> x0, waiting for transfers between devices: 29 us -> none  [the longest x1 29 us: shards(): lax.all_to_all(input_all, 'dp', split_axis=1, concat_axis=0, tiled=True)]
    dot_general x3, matrix products: 41.4 us -> 15 us  [product(): lax.dot_general(left, right, over_rows, preferred_element_type=jnp.float32)]
    unnamed x4 -> x6, local copies, waits for them, and re-layouts: 12.8 us -> 0.42 us
    all_to_all x2 -> x0, starting transfers between devices: 8.23 us -> none  [the longest x1 4.48 us: shards(): lax.all_to_all(input_all, 'dp', split_axis=1, concat_axis=0, tiled=True)]
    all_to_all x4 -> x0, local copies, waits for them, and re-layouts: 7.18 us -> none  [the longest x2 4.67 us: shards(): lax.all_to_all(input_all, 'dp', split_axis=1, concat_axis=0, tiled=True)]
    slice x1, local copies, waits for them, and re-layouts: 6.02 us -> 2.1 us  [shards(): inputs, outputs = (xg[0].reshape(total, block), xg[1].reshape(total, block))]
  transfers between devices with their start and end apart: 5 -> 0, of which waited for: 4 -> 0; matrix products, arithmetic and copies ran while one was open for 24% -> 0% of each run, Pallas kernels for 0% -> 0%
where the time goes in v1:
time: 90.7 us; the launch traced here: 90.5 us
  Pallas kernels  71.5 us (79%)
  matrix products  15 us (17%)
  local copies, waits for them, and re-layouts  2.52 us (3%)
    pallas_call x1, Pallas kernels, shards(): pl.pallas_call(functools.partial(exchange, n_dp, n_t), out_shape=(jax.Sha...  71.5 us
    dot_general x3, matrix products, product(): lax.dot_general(left, right, over_rows, preferred_element_type=jnp.float32)  15 us
    slice x1, local copies, waits for them, and re-layouts, shards(): inputs, outputs = (xg[0].reshape(total, block), xg[1].reshape(total, block))  2.1 us

profile of v1, /device:TPU:0, one launch (start us, length us, event | category | flops | bytes accessed | tf_op | source)
XLA Modules:
  0.0 90.5 jit_solution(17957963094997546497)
XLA Ops:
  0.7 0.8 fusion.spread_ref
  1.5 71.5 %shard_map.85 = (bf16[2,4,160,1024]{3,2,1,0:T(8,128)(2,1)}, bf16[4,160,2048]{2,1,0:T(8,128)(2,1)}, bf16[4,160,2048]{2,1,0:T(8,128)(2,1)}, bf16[4,160,2048]{2,1,0:T(8,128)(2,1)}) custom-call(bf16[160,512]{1,0:T(8,128)(2,1)} %bitcast.21, bf16[160,512]{1,0:T(8,128)(2,1)} %bitcast.22, bf16[160,2048]{1,0:T(8,128)(2,1)} %bitcast.19, bf16[160,2048]{1,0:T(8,128)(2,1)} %bitcast.20, ...), custom_call_target="tpu_custom_call" | custom-call | flops 2684354560 | bytes 50000000 | tf_op jit(solution)/shard_map/pallas_call | solution.py:368
  73.0 0.0 copy-start.2
  73.0 2.1 %fusion.3 = (bf16[1,4,160,1024]{3,2,1,0:T(8,128)(2,1)S(1)}, bf16[1,4,160,1024]{3,2,1,0:T(8,128)(2,1)S(1)}) fusion(bf16[2,4,160,1024]{3,2,1,0:T(8,128)(2,1)} %get-tuple-element.8), kind=kLoop, calls=%fused_computation.13 | loop fusion | bytes 5242880 | tf_op jit(solution)/shard_map/slice | solution.py:396
  75.1 0.4 copy-done.2
  75.5 0.0 copy-start.1
  75.5 5.0 %convolution_convert_fusion.2 = bf16[2048,1024]{1,0:T(8,128)(2,1)} fusion(bf16[640,2048]{1,0:T(8,128)(2,1)S(1)} %bitcast.26, bf16[640,1024]{1,0:T(8,128)(2,1)S(1)} %bitcast.18), kind=kOutput, calls=%fused_computation.2 | convolution fusion | flops 2686451712 | bytes 8126464 | tf_op jit(solution)/shard_map/dot_general | solution.py:400
  80.5 0.0 copy-done.1
  80.5 0.0 copy-start
  80.5 5.0 %convolution_convert_fusion = bf16[1024,2048]{1,0:T(8,128)(2,1)} fusion(bf16[640,1024]{1,0:T(8,128)(2,1)S(1)} %bitcast.16, bf16[640,2048]{1,0:T(8,128)(2,1)S(1)} %bitcast.25), kind=kOutput, calls=%fused_computation | convolution fusion | flops 2686451712 | bytes 8126464 | tf_op jit(solution)/shard_map/dot_general | solution.py:400
  85.5 0.0 copy-done
  85.5 5.0 %convolution_convert_fusion.1 = bf16[1024,2048]{1,0:T(8,128)(2,1)} fusion(bf16[640,1024]{1,0:T(8,128)(2,1)S(1)} %bitcast.17, bf16[640,2048]{1,0:T(8,128)(2,1)S(1)} %bitcast.24), kind=kOutput, calls=%fused_computation.1 | convolution fusion | flops 2686451712 | bytes 8126464 | tf_op jit(solution)/shard_map/dot_general | solution.py:400
  (3 shorter events, 0.0 us)
Async XLA Ops:
  73.0 2.5 %copy-start.2 = (bf16[4,160,2048]{2,1,0:T(8,128)(2,1)S(1)}, bf16[4,160,2048]{2,1,0:T(8,128)(2,1)}, u32[]{:S(2)}) copy-start(bf16[4,160,2048]{2,1,0:T(8,128)(2,1)} %get-tuple-element.7) | copy-start | bytes 7864324
  75.5 5.0 %copy-start.1 = (bf16[4,160,2048]{2,1,0:T(8,128)(2,1)S(1)}, bf16[4,160,2048]{2,1,0:T(8,128)(2,1)}, u32[]{:S(2)}) copy-start(bf16[4,160,2048]{2,1,0:T(8,128)(2,1)} %get-tuple-element.10) | copy-start | bytes 7864324
  80.5 5.0 %copy-start = (bf16[4,160,2048]{2,1,0:T(8,128)(2,1)S(1)}, bf16[4,160,2048]{2,1,0:T(8,128)(2,1)}, u32[]{:S(2)}) copy-start(bf16[4,160,2048]{2,1,0:T(8,128)(2,1)} %get-tuple-element.9) | copy-start | bytes 7864324

commit v2 on v1

--- a/solution.py
+++ b/solution.py
@@ -2,6 +2,7 @@
 
 import jax
 import jax.numpy as jnp
+import numpy as np
 from jax import lax
 from jax.experimental import pallas as pl
 from jax.experimental.pallas import tpu as pltpu
@@ -13,7 +14,7 @@
 
 
 def exchange(n_dp, n_t, out_ref, in_ref, silu_ref, up_ref, code_ref, spread_ref, w_ref,
-             xg, hid_all, gate_all, up_all,
+             xin, xout, hid_all, gate_all, up_all,
              og, wbuf, vbuf, own, stage,
              w_sem, p_send, p_recv, py_send, py_recv, og_sem,
              s_send, s_recv, h_send, h_sem, c_recv, zu_send, zd_send, y_send, y_recv,
@@ -27,6 +28,7 @@
     block = width // n_dp
     fc = hidden // CHUNKS
     units = 2 + 4 * (chips - 1)
+    xg = (xin, xout)
     all_acts = (hid_all, gate_all, up_all)
 
     d = lax.axis_index("dp")
@@ -125,7 +127,7 @@
         src = in_ref if r == 0 else stage.at[a, r - 1]
         u = unit_of(r, a) + c
         i = 0 if r == 0 else 1 + (r - 1) * 2 + a
-        dst = xg.at[a, group_from(r, c), :, at_col(chain_col if ratio == 2 else 0, cols)]
+        dst = xg[a].at[group_from(r, c), :, at_col(chain_col if ratio == 2 else 0, cols)]
         if to_self:
             return pltpu.make_async_copy(src, dst, c_recv.at[u])
         return remote(src, dst, h_send.at[i], c_recv.at[u], partner, t)
@@ -207,27 +209,14 @@
                 remote(land, land, s_send.at[a], s_recv.at[a, r - 1], partner, t).wait_recv()
             hand_start(r, a)
 
-    og_own.wait()
-    for k in range(rows):
-        side_wait(k).wait_recv()
-
-    o_own = pltpu.make_async_copy(og.at[:, at_col(d, block)], xg.at[1, d], o_sem)
-    o_own.start()
-    o_other = remote(og.at[:, at_col(partner, block)], xg.at[1, d], o_send, o_recv, partner, t)
-    o_other.start()
-
     go_up = jnp.logical_and(in_chain, jnp.logical_and(z >= head_row, z + 1 < rows))
     go_down = jnp.logical_and(in_chain, jnp.logical_and(z <= head_row, z > 0))
     z_up = lax.min(z + 1, rows - 1) * 2 + y
     z_down = lax.max(z - 1, 0) * 2 + y
 
     def unit_ref(u, col):
-        v = lax.max(u - 2, 0)
-        far_unit = u >= 2
-        r = jnp.where(far_unit, v // 4 + 1, 0)
-        a = jnp.where(far_unit, lax.rem(v // 2, 2), 0)
-        core = lax.rem(u, 2)
-        return xg.at[a, group_from(r, core), :, at_col(col, cols)]
+        r, a, core = (0, 0, u) if u < 2 else ((u - 2) // 4 + 1, (u - 2) // 2 % 2, u % 2)
+        return xg[a].at[group_from(r, core), :, at_col(col, cols)]
 
     def chain(u):
         piece = unit_ref(u, chain_col)
@@ -235,26 +224,41 @@
                 remote(piece, piece, zd_send.at[u], c_recv.at[u], d, z_down),
                 remote(piece, piece, y_send.at[u], y_recv.at[u], d, y_peer))
 
-    def chain_step(u):
+    at_head = jnp.logical_and(in_chain, z == head_row)
+    past_head = jnp.logical_and(in_chain, z != head_row)
+
+    def chain_step(u, role):
         up_copy, down_copy, across = chain(u)
 
-        @pl.when(in_chain)
+        @pl.when(role)
         def _():
             up_copy.wait_recv()
 
-        @pl.when(go_up)
+        @pl.when(jnp.logical_and(role, go_up))
         def _():
             up_copy.start()
 
-        @pl.when(go_down)
+        @pl.when(jnp.logical_and(role, go_down))
         def _():
             down_copy.start()
 
-        @pl.when(in_chain)
+        @pl.when(role)
         def _():
             across.start()
 
     per = -(-units // CHUNKS)
+
+    for u in range(units):
+        chain_step(u, at_head)
+
+    og_own.wait()
+    for k in range(rows):
+        side_wait(k).wait_recv()
+
+    o_own = pltpu.make_async_copy(og.at[:, at_col(d, block)], xg[1].at[d], o_sem)
+    o_own.start()
+    o_other = remote(og.at[:, at_col(partner, block)], xg[1].at[d], o_send, o_recv, partner, t)
+    o_other.start()
 
     def late(j, carry):
         f = f_part(j)
@@ -265,12 +269,6 @@
         own[2, :, f] = (grad * silu_ref[:, f].astype(jnp.float32)).astype(jnp.bfloat16)
         send_own(1, j)
         send_own(2, j)
-        for i in range(per):
-            u = j * per + i
-
-            @pl.when(u < units)
-            def _():
-                chain_step(u)
         return carry
 
     lax.fori_loop(0, CHUNKS, late, 0)
@@ -289,7 +287,10 @@
         relay(1)(j, carry)
         return relay(2)(j, carry)
 
-    lax.fori_loop(0, CHUNKS, relay_late, 0)
+    for j in range(CHUNKS):
+        for u in range(j * per, min((j + 1) * per, units)):
+            chain_step(u, past_head)
+        relay_late(j, 0)
 
     for k in range(1, rows):
         row_copy(k).wait_send()
@@ -311,7 +312,7 @@
     o_own.wait()
     o_other.wait()
 
-    def unit_end(u, carry):
+    def unit_end(u):
         up_copy, down_copy, across = chain(u)
 
         @pl.when(go_up)
@@ -330,9 +331,9 @@
         def _():
             piece = unit_ref(u, side_col)
             remote(piece, piece, y_send.at[u], y_recv.at[u], d, y_peer).wait_recv()
-        return carry
-
-    lax.fori_loop(0, units, unit_end, 0)
+
+    for u in range(units):
+        unit_end(u)
 
     def act_end(j, carry):
         for a in range(3):
@@ -348,15 +349,27 @@
     lax.fori_loop(0, CHUNKS, act_end, 0)
 
 
+def products(in_ref, out_ref, hid_ref, gate_ref, up_ref, down_grad, gate_grad, up_grad, turned):
+    @pl.when(pl.program_id(0) == 0)
+    def _():
+        turned[...] = in_ref[...].T
+
+    def product(left, right):
+        return jnp.dot(left, right, preferred_element_type=jnp.float32).astype(jnp.bfloat16)
+
+    gate_grad[...] = product(turned[...], gate_ref[...])
+    up_grad[...] = product(turned[...], up_ref[...])
+    down_grad[...] = product(hid_ref[...].T, out_ref[...])
+
+
 def shards(n_dp, n_t, out_grad, layer_input, w_down, silu_gate, up_proj, slope_codes):
     hidden, width = w_down.shape
     cols = out_grad.shape[2]
     tokens = out_grad.shape[0] * out_grad.shape[1]
     chips, rows, block = n_dp // 2, n_t // 2, width // n_dp
     words = tokens // 10
-    row = lax.broadcasted_iota(jnp.int32, (tokens, tokens), 0)
-    col = lax.broadcasted_iota(jnp.int32, (tokens, tokens), 1)
-    spread = (col == (row % 10) * words + row // 10).astype(jnp.bfloat16)
+    row, col = np.arange(tokens)[:, None], np.arange(tokens)[None, :]
+    spread = jnp.asarray(col == (row % 10) * words + row // 10, jnp.bfloat16)
     units = 2 + 4 * (chips - 1)
     far = chips - 1
     bf16 = jnp.bfloat16
@@ -364,12 +377,13 @@
     vmem = pl.BlockSpec(memory_space=pltpu.VMEM)
     anywhere = pl.BlockSpec(memory_space=pl.ANY)
     acts = jax.ShapeDtypeStruct((n_dp, tokens, hidden), bf16)
+    rows_of_block = jax.ShapeDtypeStruct((n_dp, tokens, block), bf16)
     flops = 2 * tokens * hidden * width
-    xg, hid, gate, up = pl.pallas_call(
+    xin, xout, hid, gate, up = pl.pallas_call(
         functools.partial(exchange, n_dp, n_t),
-        out_shape=(jax.ShapeDtypeStruct((2, n_dp, tokens, block), bf16), acts, acts, acts),
+        out_shape=(rows_of_block, rows_of_block, acts, acts, acts),
         in_specs=[vmem] * 6 + [anywhere],
-        out_specs=[anywhere] * 4,
+        out_specs=[anywhere] * 5,
         scratch_shapes=[
             pltpu.VMEM((tokens, width), bf16),
             pltpu.VMEM((hidden, width), bf16),
@@ -393,16 +407,23 @@
         slope_codes.reshape(words, hidden), spread, w_down,
     )
     total = n_dp * tokens
-    inputs, outputs = xg[0].reshape(total, block), xg[1].reshape(total, block)
-    over_rows = (((0,), (0,)), ((), ()))
-
-    def product(left, right):
-        return lax.dot_general(left, right, over_rows, preferred_element_type=jnp.float32).astype(bf16)
-
-    return (
-        product(hid.reshape(total, hidden), outputs),
-        product(inputs, gate.reshape(total, hidden)),
-        product(inputs, up.reshape(total, hidden)),
+    inputs, outputs = xin.reshape(total, block), xout.reshape(total, block)
+    piece = min(512, hidden)
+    whole = pl.BlockSpec((total, block), lambda i: (0, 0))
+    part = pl.BlockSpec((total, piece), lambda i: (0, i))
+    tall = pl.BlockSpec((block, piece), lambda i: (0, i))
+    across = jax.ShapeDtypeStruct((block, hidden), bf16)
+    return pl.pallas_call(
+        products,
+        grid=(hidden // piece,),
+        out_shape=(jax.ShapeDtypeStruct((hidden, block), bf16), across, across),
+        in_specs=[whole, whole, part, part, part],
+        out_specs=[pl.BlockSpec((piece, block), lambda i: (i, 0)), tall, tall],
+        scratch_shapes=[pltpu.VMEM((block, total), bf16)],
+        compiler_params=pltpu.CompilerParams(vmem_limit_bytes=60 * 1024 * 1024),
+    )(
+        inputs, outputs, hid.reshape(total, hidden),
+        gate.reshape(total, hidden), up.reshape(total, hidden),
     )
 
 

time: 90.7 us -> 77.3 us (0.85)
  the two profiles are of different devices: /device:TPU:0 before, /device:TPU:3 now
where the time goes in v2:
time: 77.3 us; the launch traced here: 77.1 us
  Pallas kernels  76.5 us (99%)
    pallas_call x1, Pallas kernels, shards(): pl.pallas_call(functools.partial(exchange, n_dp, n_t), out_shape=(rows_of...  62 us
    pallas_call x1, Pallas kernels, shards(): pl.pallas_call(products, grid=(hidden // piece,), out_shape=(jax.ShapeDty...  14.5 us

profile of v2, /device:TPU:3, one launch (start us, length us, event | category | flops | bytes accessed | tf_op | source)
XLA Modules:
  0.0 77.1 jit_solution(5870915271707755844)
XLA Ops:
  0.6 62.0 %shard_map.94 = (bf16[4,160,1024]{2,1,0:T(8,128)(2,1)}, bf16[4,160,1024]{2,1,0:T(8,128)(2,1)}, bf16[4,160,2048]{2,1,0:T(8,128)(2,1)}, bf16[4,160,2048]{2,1,0:T(8,128)(2,1)}, bf16[4,160,2048]{2,1,0:T(8,128)(2,1)}) custom-call(bf16[160,512]{1,0:T(8,128)(2,1)} %bitcast.17, bf16[160,512]{1,0:T(8,128)(2,1)} %bitcast.18, bf16[160,2048]{1,0:T(8,128)(2,1)} %bitcast.15, ...), custom_call_target="tpu_custom_call" | custom-call | flops 2684354560 | bytes 50000000 | tf_op jit(solution)/shard_map/pallas_call | solution.py:382
  62.6 14.5 %shard_map.95 = (bf16[2048,1024]{1,0:T(8,128)(2,1)}, bf16[1024,2048]{1,0:T(8,128)(2,1)}, bf16[1024,2048]{1,0:T(8,128)(2,1)}) custom-call(bf16[640,1024]{1,0:T(8,128)(2,1)} %bitcast.13, bf16[640,1024]{1,0:T(8,128)(2,1)} %bitcast.14, bf16[640,2048]{1,0:T(8,128)(2,1)} %bitcast.10, bf16[640,2048]{1,0:T(8,128)(2,1)} %bitcast.11, bf16[640,2048]{1,0:T(8,128)(2,1)} %bitcast.12), custom_call_target="tpu_custom_call" | custom-call | tf_op jit(solution)/shard_map/pallas_call | solution.py:416
